TPU v7x, 32 devices: a whole 2x2x4 slice. The times are simulated.
32 devices in a mesh: pw: 2 (over x), pair: 16 (over z, y, core).
Axes of the slice: x: 2, y: 2, z: 4, core: 2. Of those that a mesh axis runs over, the one named last changes fastest.
Arguments:
- valence_pairs: bfloat16 [64, 64, 8192], P('pair', None, 'pw'), may hold values from -0.59765625 to 0.59765625
- conduction_pairs: bfloat16 [16, 256, 8192], P('pair', None, 'pw'), may hold values from -0.59765625 to 0.59765625
- screening: float32 [8192], P('pw'), may hold values from 0.1 to 2
Outputs:
- kernel: float32 [64, 16, 64, 256], P('pair', None, 'pw')
All inputs are finite; a program needn't handle non-finite values.
Results may differ from a plain program's by a relative error of at most 0.0029.
Values may be sent and summed in bfloat16 or wider, within the bound.
A program may use at most 128 MiB of HBM per device.

v0:
```python
import jax
import jax.numpy as jnp
from jax import lax
from jax.sharding import PartitionSpec as P


def contract(piece, flat_right, band_dev, conduction):
    first, second, width = piece.shape
    product = lax.dot_general(
        piece.reshape(first * second, width),
        flat_right,
        (((1,), (1,)), ((), ())),
        preferred_element_type=jnp.float32,
    )
    return product.reshape(first, second, band_dev, conduction)


def route_rows(terms):
    owned = lax.all_to_all(terms, "pair", split_axis=0, concat_axis=2, tiled=True)
    return owned.transpose(0, 2, 1, 3)


def body(valence_pairs, conduction_pairs, screening):
    screened = (valence_pairs.astype(jnp.float32) * screening[None, None, :]).astype(jnp.bfloat16)
    band_dev, conduction, plane_dev = conduction_pairs.shape
    flat_local = conduction_pairs.reshape(band_dev * conduction, plane_dev)
    partial_value = contract(
        lax.all_gather(screened, "pair", axis=0, tiled=True), flat_local, band_dev, conduction
    )
    terms = lax.psum_scatter(partial_value, "pw", scatter_dimension=1, tiled=True)
    return route_rows(terms)


def solution(mesh):
    placed = (P("pair", None, "pw"), P("pair", None, "pw"), P("pw"))
    return jax.shard_map(
        body, mesh=mesh, in_specs=placed, out_specs=P("pair", None, "pw", None), check_vma=False
    )
```

profile of v0, /device:TPU:1, one launch (start us, length us, event | category | flops | bytes accessed | tf_op | source)
XLA Modules:
  0.0 314.3 jit_solution(8804609150901646009)
XLA Ops:
  6.5 0.0 copy-start
  6.5 0.0 all-gather.2.cloned.1.call-start
  6.5 3.5 %multiply_convert_fusion = bf16[4,64,4096]{2,1,0:T(8,128)(2,1)} fusion(bf16[4,64,4096]{2,1,0:T(8,128)(2,1)} %param.3, f32[4096]{0:T(1024)} %param.5), kind=kLoop, calls=%fused_computation | loop fusion | flops 3145728 | bytes 4210688 | tf_op jit(solution)/shard_map/convert_element_type | solution.py:24
  10.1 0.0 all-gather.2.cloned.1.call-update
  10.1 0.0 reduce-scatter.2.cloned.1.call-start
  10.1 170.6 %all-gather.2.cloned.1.call-done = bf16[64,64,4096]{2,1,0:T(8,128)(2,1)} async-done(((bf16[4,64,4096]{2,1,0:T(8,128)(2,1)}), bf16[64,64,4096]{2,1,0:T(8,128)(2,1)}) %all-gather.2.cloned.1.call-update) | async-done | bytes 33554448 | tf_op jit(solution)/shard_map/all_gather | solution.py:28
  180.8 0.0 copy-done
  180.8 17.2 %convolution_bitcast_fusion = f32[64,64,1,256]{3,1,0,2:T(8,128)} fusion(bf16[64,64,4096]{2,1,0:T(8,128)(2,1)} %all-gather.2.cloned.1.call-done, bf16[1,256,4096]{2,1,0:T(8,128)(2,1)S(1)} %copy-done), kind=kOutput, calls=%fused_computation.1 | convolution fusion | flops 8589934592 | bytes 39845888 | tf_op jit(solution)/shard_map/dot_general | solution.py:9
  198.0 0.0 reduce-scatter.2.cloned.1.call-update
  198.0 53.9 %reduce-scatter.2.cloned.1.call-done = f32[64,32,1,256]{3,1,0,2:T(8,128)} async-done(((f32[64,64,1,256]{3,1,0,2:T(8,128)}), f32[64,32,1,256]{3,1,0,2:T(8,128)}) %reduce-scatter.2.cloned.1.call-update) | async-done | bytes 2097168 | tf_op jit(solution)/shard_map/reduce_scatter | solution.py:30
  251.9 54.1 %all_to_all.18 = f32[64,32,1,256]{3,1,2,0:T(8,128)S(1)} all-to-all(f32[64,32,1,256]{3,1,2,0:T(8,128)} %bitcast.17), channel_id=1, replica_groups=mesh['pw'=2,'pair'=16] {'pair'}, dimensions={0} | all-to-all | bytes 4194304 | tf_op jit(solution)/shard_map/all_to_all | solution.py:19
  306.0 1.5 copy.8
Async XLA Ops:
  6.5 174.2 %copy-start = (bf16[1,256,4096]{2,1,0:T(8,128)(2,1)S(1)}, bf16[1,256,4096]{2,1,0:T(8,128)(2,1)}, u32[]{:S(2)}) copy-start(bf16[1,256,4096]{2,1,0:T(8,128)(2,1)} %param.4) | copy-start | bytes 6291460
  6.5 174.2 %all-gather.2.cloned.1.call-start = ((), (), s32[]{:S(2)}) async-start(), calls=%async_computation.2 | async-start | bytes 35651584 | tf_op jit(solution)/shard_map/all_gather | solution.py:28
  10.1 241.8 %reduce-scatter.2.cloned.1.call-start = ((), (), s32[]{:S(2)}) async-start(), calls=%async_computation.3 | async-start | bytes 6291456 | tf_op jit(solution)/shard_map/reduce_scatter | solution.py:30
Sparse Core Ops, SparseCore 0:
  10.2 170.5 all-gather.1
  198.1 53.7 reduce-scatter.1
where the time goes:
time: 314 us
  waiting for transfers between devices  225 us (72%)
  blocking collectives  54.1 us (17%)
  matrix products  17.2 us (5%)
  between operations  13.4 us (4%)
  other arithmetic  3.53 us (1%)
    all_gather x1, waiting for transfers between devices, body(): lax.all_gather(screened, 'pair', axis=0, tiled=True)  171 us
    all_to_all x1, blocking collectives, route_rows(): lax.all_to_all(terms, 'pair', split_axis=0, concat_axis=2, tiled=True)  54.1 us
    reduce_scatter x1, waiting for transfers between devices, body(): lax.psum_scatter(partial_value, 'pw', scatter_dimension=1, tiled=True)  53.9 us
    dot_general x1, matrix products, contract(): lax.dot_general(piece.reshape(first * second, width), flat_right, (((1,),...  17.2 us
  transfers between devices with their start and end apart: 2, of which 2 were waited for; matrix products, arithmetic and copies ran while one was open for 0% of the time, Pallas kernels for 0%

commit v1 on v0

--- a/solution.py
+++ b/solution.py
@@ -16,7 +16,10 @@
 
 
 def route_rows(terms):
-    owned = lax.all_to_all(terms, "pair", split_axis=0, concat_axis=2, tiled=True)
+    owned = jnp.concatenate(
+        lax.all_to_all(jnp.stack(jnp.split(terms, lax.axis_size("pair"), axis=0)), "pair", 0, 0),
+        axis=2,
+    )
     return owned.transpose(0, 2, 1, 3)
 
 

time: 314 us -> 329 us (1.048)
  local copies, waits for them, and re-layouts: 1.46 us -> 16.1 us
    unnamed x2 -> x17, local copies, waits for them, and re-layouts: 0.01 us -> 13.7 us
where the time goes in v1:
time: 329 us
  waiting for transfers between devices  225 us (68%)
  blocking collectives  53.9 us (16%)
  matrix products  17.2 us (5%)
  local copies, waits for them, and re-layouts  16.1 us (5%)
  between operations  13.5 us (4%)
  other arithmetic  3.53 us (1%)
    all_gather x1, waiting for transfers between devices, body(): lax.all_gather(screened, 'pair', axis=0, tiled=True)  171 us
    reduce_scatter x1, waiting for transfers between devices, body(): lax.psum_scatter(partial_value, 'pw', scatter_dimension=1, tiled=True)  53.9 us
    all_to_all x1, blocking collectives, route_rows(): lax.all_to_all(jnp.stack(jnp.split(terms, lax.axis_size('pair'), axis=0))...  53.9 us
    dot_general x1, matrix products, contract(): lax.dot_general(piece.reshape(first * second, width), flat_right, (((1,),...  17.2 us
    unnamed x17, local copies, waits for them, and re-layouts  13.7 us
  transfers between devices with their start and end apart: 2, of which 2 were waited for; matrix products, arithmetic and copies ran while one was open for 0% of the time, Pallas kernels for 0%

profile of v1, /device:TPU:1, one launch (start us, length us, event | category | flops | bytes accessed | tf_op | source)
XLA Modules:
  0.0 328.8 jit_solution(3767684782937142935)
XLA Ops:
  6.5 0.0 copy-start
  6.5 0.0 all-gather.2.cloned.1.call-start
  6.5 3.5 %multiply_convert_fusion = bf16[4,64,4096]{2,1,0:T(8,128)(2,1)} fusion(bf16[4,64,4096]{2,1,0:T(8,128)(2,1)} %param.3, f32[4096]{0:T(1024)} %param.5), kind=kLoop, calls=%fused_computation | loop fusion | flops 3145728 | bytes 4210688 | tf_op jit(solution)/shard_map/convert_element_type | solution.py:27
  10.1 0.0 all-gather.2.cloned.1.call-update
  10.1 0.0 reduce-scatter.2.cloned.1.call-start
  10.1 170.6 %all-gather.2.cloned.1.call-done = bf16[64,64,4096]{2,1,0:T(8,128)(2,1)} async-done(((bf16[4,64,4096]{2,1,0:T(8,128)(2,1)}), bf16[64,64,4096]{2,1,0:T(8,128)(2,1)}) %all-gather.2.cloned.1.call-update) | async-done | bytes 33554448 | tf_op jit(solution)/shard_map/all_gather | solution.py:31
  180.8 0.0 copy-done
  180.8 17.2 %convolution_bitcast_fusion = f32[64,64,1,256]{3,1,0,2:T(8,128)} fusion(bf16[64,64,4096]{2,1,0:T(8,128)(2,1)} %all-gather.2.cloned.1.call-done, bf16[1,256,4096]{2,1,0:T(8,128)(2,1)S(1)} %copy-done), kind=kOutput, calls=%fused_computation.1 | convolution fusion | flops 8589934592 | bytes 39845888 | tf_op jit(solution)/shard_map/dot_general | solution.py:9
  198.0 0.0 reduce-scatter.2.cloned.1.call-update
  198.0 53.9 %reduce-scatter.2.cloned.1.call-done = f32[64,32,1,256]{3,1,0,2:T(8,128)} async-done(((f32[64,64,1,256]{3,1,0,2:T(8,128)}), f32[64,32,1,256]{3,1,0,2:T(8,128)}) %reduce-scatter.2.cloned.1.call-update) | async-done | bytes 2097168 | tf_op jit(solution)/shard_map/reduce_scatter | solution.py:33
  251.9 0.9 fusion.16
  252.8 0.9 fusion.15
  253.8 0.9 fusion.14
  254.7 0.9 fusion.13
  255.6 0.9 fusion.12
  256.5 0.9 fusion.11
  257.4 0.9 fusion.10
  258.4 0.9 fusion.9
  259.3 0.9 fusion.8
  260.2 0.9 fusion.7
  261.1 0.9 fusion.6
  262.0 0.9 fusion.5
  263.0 0.9 fusion.4
  263.9 0.9 fusion.3
  264.8 0.9 fusion.2
  265.7 0.9 fusion.1
  266.6 53.9 %all_to_all.5 = f32[16,4,32,1,256]{4,2,1,3,0:T(8,128)S(1)} all-to-all(f32[16,4,32,1,256]{4,2,1,3,0:T(8,128)S(1)} %fusion.1), channel_id=1, replica_groups=mesh['pw'=2,'pair'=16] {'pair'}, dimensions={0} | all-to-all | bytes 4194304 | tf_op jit(solution)/shard_map/all_to_all | solution.py:20
  320.5 1.5 copy.5
Async XLA Ops:
  6.5 174.2 %copy-start = (bf16[1,256,4096]{2,1,0:T(8,128)(2,1)S(1)}, bf16[1,256,4096]{2,1,0:T(8,128)(2,1)}, u32[]{:S(2)}) copy-start(bf16[1,256,4096]{2,1,0:T(8,128)(2,1)} %param.4) | copy-start | bytes 6291460
  6.5 174.2 %all-gather.2.cloned.1.call-start = ((), (), s32[]{:S(2)}) async-start(), calls=%async_computation.2 | async-start | bytes 35651584 | tf_op jit(solution)/shard_map/all_gather | solution.py:31
  10.1 241.8 %reduce-scatter.2.cloned.1.call-start = ((), (), s32[]{:S(2)}) async-start(), calls=%async_computation.3 | async-start | bytes 6291456 | tf_op jit(solution)/shard_map/reduce_scatter | solution.py:33
Sparse Core Ops, SparseCore 0:
  10.2 170.5 all-gather.1
  198.1 53.7 reduce-scatter.1
